TPU v7x, 128 devices: a whole 4x4x4 slice. The times are simulated.
128 devices in a mesh: row: 8 (over z, y_hi), col: 16 (over x, y_lo, core).
Axes of the slice: x: 4, y: 4 (y_hi: 2, y_lo: 2; y = y_hi * 2 + y_lo), z: 4, core: 2. Of those that a mesh axis runs over, the one named last changes fastest.
Arguments:
- tri_panels: float32 [8192, 8192], P('row', 'col'), may hold values from -1 to 2, as said below
- rhs_rows: float32 [8192, 2048], P(('row', 'col')), may hold values from -6 to 6
Outputs:
- rhs_grid: float32 [8192, 2048], P('row', 'col')
Inputs may be any that keep to these rules, and one draw needn't show every extreme that they name: `tri_panels`: in L's row order the entries above the diagonal are zero and the diagonal entries are positive.
All inputs are finite; a program needn't handle non-finite values.
Results may differ from a plain program's by a relative error of at most 0.00011.
Values sent between devices are 32-bit elements; how exact they have to be, the bound alone decides.
A program may use at most 256 MiB of HBM per device.

v0:
```python
import jax
import jax.numpy as jnp
from jax import lax
from jax.sharding import PartitionSpec as P


def picked(array, axis, root):
    return lax.dynamic_index_in_dim(lax.all_gather(array, axis), root, 0, keepdims=False)


def on_device(tri_panels, rhs_rows):
    row_count = lax.axis_size("row")
    col_count = lax.axis_size("col")
    row_position = lax.axis_index("row")
    col_position = lax.axis_index("col")
    local_rows, block_size = tri_panels.shape
    blocks = local_rows // block_size
    sub_rows = block_size // col_count
    parted = rhs_rows.reshape(blocks, sub_rows, rhs_rows.shape[1])
    state_rhs = lax.all_to_all(parted, "col", split_axis=2, concat_axis=1, tiled=True)
    identity_block = jnp.eye(block_size, dtype=jnp.float32)
    own_pieces = tri_panels.reshape(blocks, block_size, block_size)
    own_diag = lax.dynamic_index_in_dim(own_pieces, col_position // row_count, 0, keepdims=False)
    own_diag = jnp.where(col_position % row_count == row_position, own_diag, identity_block)
    own_inverse = jax.scipy.linalg.solve_triangular(own_diag, identity_block, lower=True)

    def advance(state_rhs, panel_cols, inverse_block, step_index, first_slot):
        count = blocks - first_slot
        owner_row = step_index % row_count
        slot_index = step_index // row_count
        pieces = panel_cols.reshape(count, block_size, block_size)
        current = lax.dynamic_index_in_dim(state_rhs, slot_index, 0, keepdims=False)
        local_solution = jnp.dot(
            inverse_block,
            current,
            precision=lax.Precision.HIGHEST,
            preferred_element_type=jnp.float32,
        )
        solution = picked(local_solution, "row", owner_row)
        stored = jnp.where(row_position == owner_row, solution, current)
        state_rhs = lax.dynamic_update_index_in_dim(state_rhs, stored, slot_index, 0)
        global_block = (first_slot + jnp.arange(count, dtype=jnp.int32)) * row_count + row_position
        product = jnp.einsum("sij,jc->sic", pieces, solution, precision=lax.Precision.HIGHEST)
        trailing = state_rhs[first_slot:]
        trailing = jnp.where(
            (global_block > step_index)[:, None, None], trailing - product, trailing
        )
        if first_slot > 0:
            return jnp.concatenate([state_rhs[:first_slot], trailing], 0)
        return trailing

    group_count = (col_count + row_count - 1) // row_count
    everything, inverses = (
        lax.all_gather(tri_panels, "col", axis=1, tiled=True),
        lax.all_gather(own_inverse, "col", axis=1, tiled=True),
    )
    for first_slot in range(group_count):
        begin_step = first_slot * row_count
        end_step = min(begin_step + row_count, col_count)
        own_rows = everything[first_slot * block_size :]

        def upfront_step(step_index, state_rhs, own_rows=own_rows, first_slot=first_slot):
            panel_cols = lax.dynamic_slice_in_dim(own_rows, step_index * block_size, block_size, 1)
            inverse_block = lax.dynamic_slice_in_dim(
                inverses, step_index * block_size, block_size, 1
            )
            return advance(state_rhs, panel_cols, inverse_block, step_index, first_slot)

        state_rhs = lax.fori_loop(begin_step, end_step, upfront_step, state_rhs)
    return state_rhs.reshape(local_rows, state_rhs.shape[2])


def solution(mesh):
    return jax.shard_map(
        on_device,
        mesh=mesh,
        in_specs=(P("row", "col"), P(("row", "col"), None)),
        out_specs=P("row", "col"),
        check_vma=False,
    )
```

profile of v0, /device:TPU:101, one launch (start us, length us, event | category | flops | bytes accessed | tf_op | source)
XLA Modules:
  0.0 1221.0 jit_solution(3915089604845928567)
XLA Ops:
  9.3 11.7 while.33
  9.9 2.3 bitcast_dynamic-update-slice_fusion.2
  12.8 2.3 bitcast_dynamic-update-slice_fusion.2
  15.8 2.3 bitcast_dynamic-update-slice_fusion.2
  18.7 2.2 bitcast_dynamic-update-slice_fusion.2
  20.9 39.3 %custom-call.4 = f32[4,128,128]{1,2,0:T(8,128)S(1)} custom-call(f32[4,128,128]{2,1,0:T(8,128)S(1)} %get-tuple-element.290), custom_call_target="InvertDiagBlocksLowerTriangular" | custom-call | tf_op jit(solution)/shard_map/jit(_solve_triangular)/triangular_solve | solution.py:25
  68.3 2.8 reshape.83
  71.2 6.1 all-to-all-start
  77.2 13.4 %all-to-all-done = f32[16,1,8192]{2,1,0:T(1,128)S(1)} async-done(((f32[16,1,8192]{2,1,0:T(1,128)}), f32[16,1,8192]{2,1,0:T(1,128)S(1)}, u32[]{:S(2)}, u32[]{:S(2)}) %all-to-all-start) | async-done | bytes 524320 | tf_op jit(solution)/shard_map/all_to_all | solution.py:20
  91.1 1.9 reduce
  93.0 1.8 reshape.84
  95.7 90.5 %all-gather.13.cloned.1.call-done = f32[1024,8192]{1,0:T(8,128)} async-done(((f32[1024,512]{1,0:T(8,128)}), f32[1024,8192]{1,0:T(8,128)}) %all-gather.13.cloned.1.call-update) | async-done | bytes 33554448 | tf_op jit(solution)/shard_map/all_gather | solution.py:54
  186.2 11.5 slice.70
  197.7 82.6 %all-gather.11.cloned.1.call-done = f32[512,8192]{1,0:T(8,128)} async-done(((f32[512,512]{1,0:T(8,128)}), f32[512,8192]{1,0:T(8,128)}) %all-gather.11.cloned.1.call-update) | async-done | bytes 16777232 | tf_op jit(solution)/shard_map/all_gather | solution.py:55
  280.3 469.1 %while.31 = (s32[]{:T(128)}, f32[2,512,128]{2,1,0:T(8,128)S(1)}, s32[]{:T(128)}, f32[512,8192]{1,0:T(8,128)}, f32[1024,8192]{1,0:T(8,128)}, /*index=5*/s32[]{:T(...) while((s32[]{:T(128)}, f32[2,512,128]{2,1,0:T(8,128)S(1)}, ...), condition=%wide.region_1.2_spmd, body=%wide.region_0.1_spmd.sunk | while | flops 1208287232 | bytes 17039816 | solution.py:69
  280.3 2.9 fusion.63
  285.0 50.1 %all-gather.15.cloned.1.call-done = f32[4096,128]{1,0:T(8,128)} async-done(((f32[512,128]{1,0:T(8,128)}), f32[4096,128]{1,0:T(8,128)}) %all-gather.15.cloned.1.call-update) | async-done | bytes 2097168 | tf_op jit(solution)/shard_map/while/body/eval_jaxpr/all_gather | solution.py:8
  336.1 3.0 fusion.64
  339.2 2.9 fusion.63
  343.9 49.8 %all-gather.15.cloned.1.call-done = f32[4096,128]{1,0:T(8,128)} async-done(((f32[512,128]{1,0:T(8,128)}), f32[4096,128]{1,0:T(8,128)}) %all-gather.15.cloned.1.call-update) | async-done | bytes 2097168 | tf_op jit(solution)/shard_map/while/body/eval_jaxpr/all_gather | solution.py:8
  394.7 3.0 fusion.64
  397.8 2.9 fusion.63
  402.5 49.8 %all-gather.15.cloned.1.call-done = f32[4096,128]{1,0:T(8,128)} async-done(((f32[512,128]{1,0:T(8,128)}), f32[4096,128]{1,0:T(8,128)}) %all-gather.15.cloned.1.call-update) | async-done | bytes 2097168 | tf_op jit(solution)/shard_map/while/body/eval_jaxpr/all_gather | solution.py:8
  453.3 3.0 fusion.64
  456.4 2.9 fusion.63
  461.1 49.8 %all-gather.15.cloned.1.call-done = f32[4096,128]{1,0:T(8,128)} async-done(((f32[512,128]{1,0:T(8,128)}), f32[4096,128]{1,0:T(8,128)}) %all-gather.15.cloned.1.call-update) | async-done | bytes 2097168 | tf_op jit(solution)/shard_map/while/body/eval_jaxpr/all_gather | solution.py:8
  511.9 3.0 fusion.64
  515.0 2.9 fusion.63
  519.7 49.8 %all-gather.15.cloned.1.call-done = f32[4096,128]{1,0:T(8,128)} async-done(((f32[512,128]{1,0:T(8,128)}), f32[4096,128]{1,0:T(8,128)}) %all-gather.15.cloned.1.call-update) | async-done | bytes 2097168 | tf_op jit(solution)/shard_map/while/body/eval_jaxpr/all_gather | solution.py:8
  570.6 3.0 fusion.64
  573.6 2.9 fusion.63
  578.4 49.8 %all-gather.15.cloned.1.call-done = f32[4096,128]{1,0:T(8,128)} async-done(((f32[512,128]{1,0:T(8,128)}), f32[4096,128]{1,0:T(8,128)}) %all-gather.15.cloned.1.call-update) | async-done | bytes 2097168 | tf_op jit(solution)/shard_map/while/body/eval_jaxpr/all_gather | solution.py:8
  629.2 3.0 fusion.64
  632.2 2.9 fusion.63
  637.0 49.8 %all-gather.15.cloned.1.call-done = f32[4096,128]{1,0:T(8,128)} async-done(((f32[512,128]{1,0:T(8,128)}), f32[4096,128]{1,0:T(8,128)}) %all-gather.15.cloned.1.call-update) | async-done | bytes 2097168 | tf_op jit(solution)/shard_map/while/body/eval_jaxpr/all_gather | solution.py:8
  687.8 3.0 fusion.64
  690.9 2.9 fusion.63
  695.6 49.8 %all-gather.15.cloned.1.call-done = f32[4096,128]{1,0:T(8,128)} async-done(((f32[512,128]{1,0:T(8,128)}), f32[4096,128]{1,0:T(8,128)}) %all-gather.15.cloned.1.call-update) | async-done | bytes 2097168 | tf_op jit(solution)/shard_map/while/body/eval_jaxpr/all_gather | solution.py:8
  746.4 3.0 fusion.64
  749.4 464.0 %while.32 = (s32[]{:T(128)}, f32[2,512,128]{2,1,0:T(8,128)S(1)}, s32[]{:T(128)}, f32[512,8192]{1,0:T(8,128)}, s32[1]{0:T(128)}, /*index=5*/f32[512,8192]{1,0:T(8...) while((s32[]{:T(128)}, f32[2,512,128]{2,1,0:T(8,128)S(1)}, ...), condition=%wide.region_3.4_spmd, body=%wide.region_2.3_spmd.sunk | while | flops 805634048 | bytes 12846105 | solution.py:69
  749.5 2.9 fusion.69
  752.5 51.6 %all-gather.17.cloned.1.call-done = f32[4096,128]{1,0:T(8,128)} async-done(((f32[512,128]{1,0:T(8,128)}), f32[4096,128]{1,0:T(8,128)}) %all-gather.17.cloned.1.call-update) | async-done | bytes 2097168 | tf_op jit(solution)/shard_map/while/body/eval_jaxpr/all_gather | solution.py:8
  805.1 2.3 fusion.70
  807.5 2.9 fusion.69
  810.5 51.6 %all-gather.17.cloned.1.call-done = f32[4096,128]{1,0:T(8,128)} async-done(((f32[512,128]{1,0:T(8,128)}), f32[4096,128]{1,0:T(8,128)}) %all-gather.17.cloned.1.call-update) | async-done | bytes 2097168 | tf_op jit(solution)/shard_map/while/body/eval_jaxpr/all_gather | solution.py:8
  863.1 2.3 fusion.70
  865.5 2.9 fusion.69
  868.5 51.6 %all-gather.17.cloned.1.call-done = f32[4096,128]{1,0:T(8,128)} async-done(((f32[512,128]{1,0:T(8,128)}), f32[4096,128]{1,0:T(8,128)}) %all-gather.17.cloned.1.call-update) | async-done | bytes 2097168 | tf_op jit(solution)/shard_map/while/body/eval_jaxpr/all_gather | solution.py:8
  921.1 2.3 fusion.70
  923.5 2.9 fusion.69
  926.5 51.6 %all-gather.17.cloned.1.call-done = f32[4096,128]{1,0:T(8,128)} async-done(((f32[512,128]{1,0:T(8,128)}), f32[4096,128]{1,0:T(8,128)}) %all-gather.17.cloned.1.call-update) | async-done | bytes 2097168 | tf_op jit(solution)/shard_map/while/body/eval_jaxpr/all_gather | solution.py:8
  979.1 2.3 fusion.70
  981.5 2.9 fusion.69
  984.5 51.6 %all-gather.17.cloned.1.call-done = f32[4096,128]{1,0:T(8,128)} async-done(((f32[512,128]{1,0:T(8,128)}), f32[4096,128]{1,0:T(8,128)}) %all-gather.17.cloned.1.call-update) | async-done | bytes 2097168 | tf_op jit(solution)/shard_map/while/body/eval_jaxpr/all_gather | solution.py:8
  1037.1 2.3 fusion.70
  1039.5 2.9 fusion.69
  1042.5 51.6 %all-gather.17.cloned.1.call-done = f32[4096,128]{1,0:T(8,128)} async-done(((f32[512,128]{1,0:T(8,128)}), f32[4096,128]{1,0:T(8,128)}) %all-gather.17.cloned.1.call-update) | async-done | bytes 2097168 | tf_op jit(solution)/shard_map/while/body/eval_jaxpr/all_gather | solution.py:8
  1095.1 2.3 fusion.70
  1097.5 2.9 fusion.69
  1100.5 51.6 %all-gather.17.cloned.1.call-done = f32[4096,128]{1,0:T(8,128)} async-done(((f32[512,128]{1,0:T(8,128)}), f32[4096,128]{1,0:T(8,128)}) %all-gather.17.cloned.1.call-update) | async-done | bytes 2097168 | tf_op jit(solution)/shard_map/while/body/eval_jaxpr/all_gather | solution.py:8
  1153.1 2.3 fusion.70
  1155.5 2.9 fusion.69
  1158.5 51.6 %all-gather.17.cloned.1.call-done = f32[4096,128]{1,0:T(8,128)} async-done(((f32[512,128]{1,0:T(8,128)}), f32[4096,128]{1,0:T(8,128)}) %all-gather.17.cloned.1.call-update) | async-done | bytes 2097168 | tf_op jit(solution)/shard_map/while/body/eval_jaxpr/all_gather | solution.py:8
  1211.1 2.3 fusion.70
  (115 shorter events, 46.8 us)
Async XLA Ops:
  6.5 1.6 copy-start.1
  6.5 179.6 %all-gather.13.cloned.1.call-start = ((), (), s32[]{:S(2)}) async-start(), calls=%async_computation.2 | async-start | bytes 35651584 | tf_op jit(solution)/shard_map/all_gather | solution.py:54
  7.3 273.0 %all-gather.11.cloned.1.call-start = ((), (), s32[]{:S(2)}) async-start(), calls=%async_computation.1 | async-start | bytes 17825792 | tf_op jit(solution)/shard_map/all_gather | solution.py:55
  65.8 1.5 copy-start.2
  71.2 19.5 %all-to-all-start = ((f32[16,1,8192]{2,1,0:T(1,128)}), f32[16,1,8192]{2,1,0:T(1,128)S(1)}, u32[]{:S(2)}, u32[]{:S(2)}) async-start(f32[16,1,8192]{2,1,0:T(1,128)} %reshape.83), calls=%async_computation | async-start | bytes 1048576 | tf_op jit(solution)/shard_map/all_to_all | solution.py:20
  280.3 54.9 %all-gather.15.cloned.1.call-start = ((), (), s32[]{:S(2)}) async-start(), calls=%async_computation.3 | async-start | bytes 2359296 | tf_op jit(solution)/shard_map/while/body/eval_jaxpr/all_gather | solution.py:8
  339.1 54.6 %all-gather.15.cloned.1.call-start = ((), (), s32[]{:S(2)}) async-start(), calls=%async_computation.3 | async-start | bytes 2359296 | tf_op jit(solution)/shard_map/while/body/eval_jaxpr/all_gather | solution.py:8
  397.7 54.6 %all-gather.15.cloned.1.call-start = ((), (), s32[]{:S(2)}) async-start(), calls=%async_computation.3 | async-start | bytes 2359296 | tf_op jit(solution)/shard_map/while/body/eval_jaxpr/all_gather | solution.py:8
  456.3 54.6 %all-gather.15.cloned.1.call-start = ((), (), s32[]{:S(2)}) async-start(), calls=%async_computation.3 | async-start | bytes 2359296 | tf_op jit(solution)/shard_map/while/body/eval_jaxpr/all_gather | solution.py:8
  514.9 54.7 %all-gather.15.cloned.1.call-start = ((), (), s32[]{:S(2)}) async-start(), calls=%async_computation.3 | async-start | bytes 2359296 | tf_op jit(solution)/shard_map/while/body/eval_jaxpr/all_gather | solution.py:8
  573.5 54.6 %all-gather.15.cloned.1.call-start = ((), (), s32[]{:S(2)}) async-start(), calls=%async_computation.3 | async-start | bytes 2359296 | tf_op jit(solution)/shard_map/while/body/eval_jaxpr/all_gather | solution.py:8
  632.2 54.7 %all-gather.15.cloned.1.call-start = ((), (), s32[]{:S(2)}) async-start(), calls=%async_computation.3 | async-start | bytes 2359296 | tf_op jit(solution)/shard_map/while/body/eval_jaxpr/all_gather | solution.py:8
  690.8 54.6 %all-gather.15.cloned.1.call-start = ((), (), s32[]{:S(2)}) async-start(), calls=%async_computation.3 | async-start | bytes 2359296 | tf_op jit(solution)/shard_map/while/body/eval_jaxpr/all_gather | solution.py:8
  749.4 54.7 %all-gather.17.cloned.1.call-start = ((), (), s32[]{:S(2)}) async-start(), calls=%async_computation.4 | async-start | bytes 2359296 | tf_op jit(solution)/shard_map/while/body/eval_jaxpr/all_gather | solution.py:8
  807.4 54.6 %all-gather.17.cloned.1.call-start = ((), (), s32[]{:S(2)}) async-start(), calls=%async_computation.4 | async-start | bytes 2359296 | tf_op jit(solution)/shard_map/while/body/eval_jaxpr/all_gather | solution.py:8
  865.4 54.7 %all-gather.17.cloned.1.call-start = ((), (), s32[]{:S(2)}) async-start(), calls=%async_computation.4 | async-start | bytes 2359296 | tf_op jit(solution)/shard_map/while/body/eval_jaxpr/all_gather | solution.py:8
  923.4 54.6 %all-gather.17.cloned.1.call-start = ((), (), s32[]{:S(2)}) async-start(), calls=%async_computation.4 | async-start | bytes 2359296 | tf_op jit(solution)/shard_map/while/body/eval_jaxpr/all_gather | solution.py:8
  981.4 54.6 %all-gather.17.cloned.1.call-start = ((), (), s32[]{:S(2)}) async-start(), calls=%async_computation.4 | async-start | bytes 2359296 | tf_op jit(solution)/shard_map/while/body/eval_jaxpr/all_gather | solution.py:8
  1039.4 54.6 %all-gather.17.cloned.1.call-start = ((), (), s32[]{:S(2)}) async-start(), calls=%async_computation.4 | async-start | bytes 2359296 | tf_op jit(solution)/shard_map/while/body/eval_jaxpr/all_gather | solution.py:8
  1097.4 54.6 %all-gather.17.cloned.1.call-start = ((), (), s32[]{:S(2)}) async-start(), calls=%async_computation.4 | async-start | bytes 2359296 | tf_op jit(solution)/shard_map/while/body/eval_jaxpr/all_gather | solution.py:8
  1155.4 54.6 %all-gather.17.cloned.1.call-start = ((), (), s32[]{:S(2)}) async-start(), calls=%async_computation.4 | async-start | bytes 2359296 | tf_op jit(solution)/shard_map/while/body/eval_jaxpr/all_gather | solution.py:8
  1213.4 0.8 copy-start
Sparse Core Ops, SparseCore 0:
  9.0 177.1 all-gather.12
  187.8 92.3 all-gather.10
  283.4 51.6 all-gather.14
  342.3 51.4 all-gather.14
  400.9 51.4 all-gather.14
  459.5 51.4 all-gather.14
  518.1 51.4 all-gather.14
  576.7 51.4 all-gather.14
  635.3 51.4 all-gather.14
  693.9 51.4 all-gather.14
  752.6 51.4 all-gather.16
  810.6 51.4 all-gather.16
  868.6 51.4 all-gather.16
  926.6 51.4 all-gather.16
  984.6 51.4 all-gather.16
  1042.6 51.4 all-gather.16
  1100.5 51.4 all-gather.16
  1158.5 51.4 all-gather.16
where the time goes:
time: 1230 us; the launch traced here: 1220 us
  waiting for transfers between devices  999 us (81%)
  matrix products  94.2 us (8%)
  other arithmetic  59.8 us (5%)
  local copies, waits for them, and re-layouts  45.9 us (4%)
  between operations  13.6 us (1%)
    all_gather x16, waiting for transfers between devices, picked(): lax.all_gather(array, axis)  812 us
    all_gather x1, waiting for transfers between devices, on_device(): lax.all_gather(tri_panels, 'col', axis=1, tiled=True)  90.5 us
    all_gather x1, waiting for transfers between devices, on_device(): lax.all_gather(own_inverse, 'col', axis=1, tiled=True)  82.6 us
    dot_general x16, matrix products, advance(): jnp.dot(inverse_block, current, precision=lax.Precision.HIGHEST, preferre...  46.7 us
    dot_general x16, matrix products, advance(): jnp.einsum('sij,jc->sic', pieces, solution, precision=lax.Precision.HIGHEST)  41.8 us
    another operation x4, other arithmetic, on_device(): jax.scipy.linalg.solve_triangular(own_diag, identity_block, lower=True)  41.5 us
  transfers between devices with their start and end apart: 19, of which 19 were waited for; matrix products, arithmetic and copies ran while one was open for 8% of the time, Pallas kernels for 0%

commit v1 on v0

v1 whole, which is shorter than its diff:
```python
import functools

import jax
import jax.numpy as jnp
from jax import lax
from jax.experimental import pallas as pl
from jax.experimental.pallas import tpu as pltpu
from jax.sharding import PartitionSpec as P

MESH = pl.DeviceIdType.MESH
F32 = jnp.float32
PIECES = 2
HIGH = lax.Precision.HIGHEST


def split(a):
    top = a.astype(jnp.bfloat16)
    return top, (a - top.astype(F32)).astype(jnp.bfloat16)


def product(a, b):
    a_top, a_rest = split(a)
    b_top, b_rest = split(b)
    dot = functools.partial(jnp.dot, preferred_element_type=F32)
    return dot(a_top, b_top) + (dot(a_top, b_rest) + dot(a_rest, b_top))


def exact(a, b):
    return jnp.dot(a, b, precision=HIGH, preferred_element_type=F32)


def invert(a_ref, w_ref):
    size = a_ref.shape[0]
    base = min(32, size)
    group = min(128, size)
    w_ref[...] = jnp.zeros_like(w_ref)
    eye = (
        lax.broadcasted_iota(jnp.int32, (base, base), 0)
        == lax.broadcasted_iota(jnp.int32, (base, base), 1)
    )
    for first in range(0, size, group):
        spots = list(range(first, first + group, base))
        scaled, scales, solved = [], [], []
        for spot in spots:
            a = a_ref[spot : spot + base, spot : spot + base]
            diag = jnp.where(eye, a, 0.0)
            inv_col = 1.0 / jnp.sum(diag, axis=1, keepdims=True)
            scales.append(1.0 / jnp.sum(diag, axis=0, keepdims=True))
            scaled.append(jnp.where(eye, 0.0, a * inv_col))
            solved.append(jnp.where(eye, jnp.ones((), F32), jnp.zeros((), F32)))
        for i in range(base - 1):
            for n in range(len(spots)):
                solved[n] = solved[n] - scaled[n][:, i : i + 1] * solved[n][i : i + 1, :]
        for n, spot in enumerate(spots):
            w_ref[spot : spot + base, spot : spot + base] = solved[n] * scales[n]
    half = base
    while half < group:
        i = lax.broadcasted_iota(jnp.int32, (group, group), 0) // half
        j = lax.broadcasted_iota(jnp.int32, (group, group), 1) // half
        mask = jnp.logical_and(i % 2 == 1, j == i - 1)
        for first in range(0, size, group):
            at = slice(first, first + group)
            w = w_ref[at, at]
            w_ref[at, at] = w - exact(w, exact(jnp.where(mask, a_ref[at, at], 0.0), w))
        half *= 2
    while half < size:
        for first in range(0, size, 2 * half):
            top = slice(first, first + half)
            low = slice(first + half, first + 2 * half)
            w_ref[low, top] = -exact(w_ref[low, low], exact(a_ref[low, top], w_ref[top, top]))
        half *= 2


def kernel(
    tri, rhs, out,
    grid, own, moved, inverse, solved, state,
    own_sem, rhs_send, rhs_recv, move_send, move_recv,
    grid_recv, source_send, pass_send,
    solved_send, solved_recv, solved_pass, out_send, out_recv,
):
    nb = own.shape[1]
    ncol = state.shape[2]
    sub = nb // 16
    part = nb // PIECES
    row = lax.axis_index("row")
    col = lax.axis_index("col")
    z, h = row // 2, row % 2
    x, low, q = col // 4, (col // 2) % 2, col % 2
    y = 2 * h + low
    first_row = 2 * z + q
    second_row = 14 - 2 * z + q

    def device(z_to, x_to, y_to, core):
        return {"row": 2 * z_to + y_to // 2, "col": 4 * x_to + 2 * (y_to % 2) + core}

    def remote(src, dst, send, recv, target):
        return pltpu.make_async_remote_copy(
            src_ref=src, dst_ref=dst, send_sem=send, recv_sem=recv,
            device_id=target, device_id_type=MESH,
        )

    here = device(z, x, y, q)

    loads = [
        pltpu.make_async_copy(tri.at[pl.ds(j * nb, nb), :], own.at[j], own_sem.at[j])
        for j in range(2)
    ]
    for load in loads:
        load.start()

    def rhs_copy(j, c_to):
        x_to, low_to, h_to = c_to // 4, (c_to // 2) % 2, c_to % 2
        src = rhs.at[pl.ds(j * sub, sub), pl.ds(pl.multiple_of(c_to * ncol, ncol), ncol)]
        dst = state.at[j, pl.ds(pl.multiple_of(col * sub, sub), sub), :]
        z_to = z if j == 0 else 3 - z
        return remote(
            src, dst, rhs_send.at[j, c_to], rhs_recv.at[j],
            device(z_to, x_to, 2 * h_to + low_to, h),
        ), pltpu.make_async_copy(src, dst, rhs_recv.at[j])

    chip = 4 * x + 2 * low + h

    def rhs_stays(j, c_to):
        return jnp.logical_and(j == 0, jnp.logical_and(c_to == chip, q == h))

    for j in range(2):

        @pl.loop(0, 16)
        def _(step, j=j):
            c_to = (step + chip) % 16
            away, home = rhs_copy(j, c_to)
            stays = rhs_stays(j, c_to)

            @pl.when(stays)
            def _():
                home.start()

            @pl.when(jnp.logical_not(stays))
            def _():
                away.start()

    for load in loads:
        load.wait()

    is_diag = col % 8 == row
    diag_slot = col // 8

    move = remote(own.at[1], moved, move_send, move_recv, device(3 - z, x, y, q))
    move_needed = col <= 8 + row
    moved_needed = col <= 14 - 2 * z + h
    early = jnp.logical_and(move_needed, jnp.logical_not(jnp.logical_and(is_diag, diag_slot == 1)))
    late = jnp.logical_and(is_diag, diag_slot == 1)

    @pl.when(early)
    def _():
        move.start()


    def sends(piece, k, dx, dy):
        par = (k // 2 + k) % 2
        first_is_y = piece % 2 == 0
        da, db = (dy, dx) if first_is_y else (dx, dy)
        on_line = db == 0
        first_plus = jnp.logical_and(on_line, jnp.logical_or(da == 0, jnp.logical_and(da == 1, par == 0)))
        first_minus = jnp.logical_and(on_line, jnp.logical_or(da == 0, jnp.logical_and(da == 3, par == 1)))
        second_plus = jnp.logical_or(on_line, jnp.logical_and(db == 1, par == 0))
        second_minus = jnp.logical_or(on_line, jnp.logical_and(db == 3, par == 1))
        if first_is_y:
            return second_plus, second_minus, first_plus, first_minus
        return first_plus, first_minus, second_plus, second_minus

    def neighbour(way, core):
        if way == 0:
            return device(z, (x + 1) % 4, y, core)
        if way == 1:
            return device(z, (x + 3) % 4, y, core)
        if way == 2:
            return device(z, x, (y + 1) % 4, core)
        return device(z, x, (y + 3) % 4, core)

    def rows_of(piece):
        return pl.ds(piece * part, part)

    def source_copies(j):
        src = own.at[0] if j == 0 else moved
        for piece in range(PIECES):
            for way in range(5):
                target = neighbour(way, h) if way < 4 else device(z, x, y, h)
                yield way, remote(
                    src.at[rows_of(piece), :],
                    grid.at[j, col, rows_of(piece), :],
                    source_send.at[j, piece, way],
                    grid_recv.at[j, col, piece],
                    target,
                )

    def source(j):
        for way, copy in source_copies(j):
            if way < 4:
                copy.start()
            else:

                @pl.when(q != h)
                def _(copy=copy):
                    copy.start()

        @pl.when(q == h)
        def _():
            grid[j, col] = own[0] if j == 0 else moved[...]

    def source_wait(j):
        for way, copy in source_copies(j):
            if way < 4:
                copy.wait_send()
            else:

                @pl.when(q != h)
                def _(copy=copy):
                    copy.wait_send()

    source_first = col <= row

    @pl.when(jnp.logical_and(source_first, jnp.logical_not(is_diag)))
    def _():
        source(0)

    @pl.when(is_diag)
    def _():
        invert(own.at[diag_slot], inverse)
        own[diag_slot] = inverse[...]

    @pl.when(late)
    def _():
        move.start()

    @pl.when(jnp.logical_and(source_first, is_diag))
    def _():
        source(0)

    def passing(j, k, do):
        dx = (x - k // 4 + 4) % 4
        dy = (y - 2 * q - (k // 2) % 2 + 4) % 4
        at_source = jnp.logical_and(dx == 0, dy == 0)
        is_source = jnp.logical_and(at_source, k % 2 == q)
        for piece in range(PIECES):
            spot = grid.at[j, k, rows_of(piece), :]
            copies = [
                remote(spot, spot, pass_send.at[j, k, piece, way], grid_recv.at[j, k, piece], neighbour(way, q))
                for way in range(4)
            ]
            flags = sends(piece, k, dx, dy)
            if do == "pass":

                @pl.when(jnp.logical_not(is_source))
                def _(copies=copies):
                    copies[0].wait_recv()

            for way in range(4):

                @pl.when(jnp.logical_and(flags[way], jnp.logical_not(at_source)))
                def _(copy=copies[way]):
                    if do == "pass":
                        copy.start()
                    else:
                        copy.wait_send()

    @pl.loop(0, first_row + 1)
    def _(k):
        passing(0, k, "pass")

    @pl.when(moved_needed)
    def _():
        move.wait_recv()
        source(1)

    @pl.loop(0, second_row + 1)
    def _(k):
        passing(1, k, "pass")

    for j in range(2):
        remote(state.at[j], state.at[j], rhs_send.at[j, 0], rhs_recv.at[j], here).wait_recv()

    def owner_z(k):
        return jnp.where(k < 8, k // 2, 7 - k // 2)

    def wanted(k, z_to):
        return jnp.logical_or(k < 8, z_to < owner_z(k))

    def solved_copies(k):
        spot = solved.at[k]
        partner_wants = jnp.logical_or(k % 2 == 0, k < 8)
        result = []
        for way in range(4):
            if way == 0:
                target, flag = device(z, x, y, 1 - q), partner_wants
            else:
                z_to = (z + (1, 3, 2)[way - 1]) % 4
                target, flag = device(z_to, x, y, 0), wanted(k, z_to)
            result.append((flag, remote(spot, spot, solved_send.at[k, way], solved_recv.at[k], target)))
        return result

    def out_copy(k):
        spot = out.at[pl.ds(pl.multiple_of((k // 8) * nb, nb), nb), :]
        stays = jnp.logical_and(k < 8, h == q)
        target = device((k % 8) // 2, x, 2 * q + low, h)
        away = remote(solved.at[k], spot, out_send.at[k // 8], out_recv.at[k // 8], target)
        home = pltpu.make_async_copy(solved.at[k], spot, out_recv.at[k // 8])
        return stays, away, home

    def is_owner(k):
        return jnp.logical_and(owner_z(k) == z, k % 2 == q)

    def pass_to_partner(k):
        spot = solved.at[k]
        flag = jnp.logical_and(q == 0, jnp.logical_and(owner_z(k) != z, wanted(k, z)))
        return flag, remote(spot, spot, solved_pass.at[k], solved_recv.at[k], device(z, x, y, 1))

    def gets(k):
        same_chip = owner_z(k) == z
        other_core = jnp.logical_and(same_chip, jnp.logical_and(k % 2 != q, jnp.logical_or(k % 2 == 0, k < 8)))
        return jnp.logical_or(other_core, jnp.logical_and(jnp.logical_not(same_chip), wanted(k, z)))

    @pl.loop(0, 16)
    def _(k):
        slot = k // 8

        @pl.when(is_owner(k))
        def _():
            solved[k] = product(grid[slot, k], state[slot])
            for flag, copy in solved_copies(k):

                @pl.when(flag)
                def _(copy=copy):
                    copy.start()

            stays, away, home = out_copy(k)

            @pl.when(stays)
            def _():
                home.start()

            @pl.when(jnp.logical_not(stays))
            def _():
                away.start()

        @pl.when(gets(k))
        def _():
            spot = solved.at[k]
            remote(spot, spot, solved_pass.at[k], solved_recv.at[k], here).wait_recv()
            flag, copy = pass_to_partner(k)

            @pl.when(flag)
            def _():
                copy.start()

        @pl.when(k < first_row)
        def _():
            state[0] = state[0] - product(grid[0, k], solved[k])

        @pl.when(k < second_row)
        def _():
            state[1] = state[1] - product(grid[1, k], solved[k])

    @pl.loop(0, 16)
    def _(k):
        @pl.when(is_owner(k))
        def _():
            for flag, copy in solved_copies(k):

                @pl.when(flag)
                def _(copy=copy):
                    copy.wait_send()

            stays, away, _ = out_copy(k)

            @pl.when(jnp.logical_not(stays))
            def _():
                away.wait_send()

        flag, copy = pass_to_partner(k)

        @pl.when(flag)
        def _():
            copy.wait_send()

        @pl.when(k <= first_row)
        def _():
            passing(0, k, "done")

        @pl.when(k <= second_row)
        def _():
            passing(1, k, "done")

    @pl.when(source_first)
    def _():
        source_wait(0)

    @pl.when(moved_needed)
    def _():
        source_wait(1)

    @pl.when(move_needed)
    def _():
        move.wait_send()

    for j in range(2):

        @pl.loop(0, 16)
        def _(c_to, j=j):
            away, _ = rhs_copy(j, c_to)

            @pl.when(jnp.logical_not(rhs_stays(j, c_to)))
            def _():
                away.wait_send()

        spot = out.at[pl.ds(j * nb, nb), :]
        remote(solved.at[0], spot, out_send.at[j], out_recv.at[j], here).wait_recv()


def on_device(tri, rhs):
    nb = tri.shape[1]
    ncol = rhs.shape[1] // 16
    dma = pltpu.SemaphoreType.DMA
    return pl.pallas_call(
        kernel,
        out_shape=jax.ShapeDtypeStruct((2 * nb, ncol), F32),
        in_specs=[pl.BlockSpec(memory_space=pl.ANY)] * 2,
        out_specs=pl.BlockSpec(memory_space=pl.ANY),
        scratch_shapes=[
            pltpu.VMEM((2, 16, nb, nb), F32),
            pltpu.VMEM((2, nb, nb), F32),
            pltpu.VMEM((nb, nb), F32),
            pltpu.VMEM((nb, nb), F32),
            pltpu.VMEM((16, nb, ncol), F32),
            pltpu.VMEM((2, nb, ncol), F32),
            dma((2,)),
            dma((2, 16)),
            dma((2,)),
            dma,
            dma,
            dma((2, 16, PIECES)),
            dma((2, PIECES, 5)),
            dma((2, 16, PIECES, 4)),
            dma((16, 4)),
            dma((16,)),
            dma((16,)),
            dma((2,)),
            dma((2,)),
        ],
        compiler_params=pltpu.CompilerParams(
            has_side_effects=True, vmem_limit_bytes=60 * 1024 * 1024
        ),
    )(tri, rhs)


def solution(mesh):
    return jax.shard_map(
        on_device,
        mesh=mesh,
        in_specs=(P("row", "col"), P(("row", "col"), None)),
        out_specs=P("row", "col"),
        check_vma=False,
    )
```

time: 1230 us -> 384 us (0.31)
  the two profiles are of different devices: /device:TPU:101 before, /device:TPU:27 now
where the time goes in v1:
time: 384 us; the launch traced here: 383 us
  Pallas kernels  381 us (99%)
    pallas_call x1, Pallas kernels, on_device(): pl.pallas_call(kernel, out_shape=jax.ShapeDtypeStruct((2 * nb, ncol), F32...  381 us

profile of v1, /device:TPU:27, one launch (start us, length us, event | category | flops | bytes accessed | tf_op | source)
XLA Modules:
  0.0 383.3 jit_solution(11847560049374431877)
XLA Ops:
  0.0 381.5 %shard_map.28 = f32[1024,128]{1,0:T(8,128)} custom-call(f32[1024,512]{1,0:T(8,128)} %tri.1, f32[64,2048]{1,0:T(8,128)} %rhs.1), custom_call_target="tpu_custom_call" | custom-call | tf_op jit(solution)/shard_map/pallas_call | solution.py:424
  381.5 1.9 copy.4

commit v2 on v1

--- a/solution.py
+++ b/solution.py
@@ -9,7 +9,8 @@
 
 MESH = pl.DeviceIdType.MESH
 F32 = jnp.float32
-PIECES = 2
+PIECES = 4
+FIRST_Y = (True, False, True, False)
 HIGH = lax.Precision.HIGHEST
 
 
@@ -73,8 +74,8 @@
 
 def kernel(
     tri, rhs, out,
-    grid, own, moved, inverse, solved, state,
-    own_sem, rhs_send, rhs_recv, move_send, move_recv,
+    grid, own, inverse, solved, state,
+    own_sem, rhs_send, rhs_recv,
     grid_recv, source_send, pass_send,
     solved_send, solved_recv, solved_pass, out_send, out_recv,
 ):
@@ -88,7 +89,7 @@
     x, low, q = col // 4, (col // 2) % 2, col % 2
     y = 2 * h + low
     first_row = 2 * z + q
-    second_row = 14 - 2 * z + q
+    second_row = 8 + first_row
 
     def device(z_to, x_to, y_to, core):
         return {"row": 2 * z_to + y_to // 2, "col": 4 * x_to + 2 * (y_to % 2) + core}
@@ -100,6 +101,20 @@
         )
 
     here = device(z, x, y, q)
+
+    barrier = pltpu.get_barrier_semaphore()
+
+    def greet(target):
+        pl.semaphore_signal(barrier, inc=1, device_id=target, device_id_type=MESH)
+
+    @pl.loop(1, 32)
+    def _(step):
+        other = (16 * h + col + step) % 32
+        greet({"row": 2 * z + other // 16, "col": other % 16})
+
+    for step in range(1, 4):
+        for core in range(2):
+            greet(device((z + step) % 4, x, y, core))
 
     loads = [
         pltpu.make_async_copy(tri.at[pl.ds(j * nb, nb), :], own.at[j], own_sem.at[j])
@@ -108,20 +123,21 @@
     for load in loads:
         load.start()
 
+    pl.semaphore_wait(barrier, 37)
+
     def rhs_copy(j, c_to):
         x_to, low_to, h_to = c_to // 4, (c_to // 2) % 2, c_to % 2
         src = rhs.at[pl.ds(j * sub, sub), pl.ds(pl.multiple_of(c_to * ncol, ncol), ncol)]
         dst = state.at[j, pl.ds(pl.multiple_of(col * sub, sub), sub), :]
-        z_to = z if j == 0 else 3 - z
         return remote(
             src, dst, rhs_send.at[j, c_to], rhs_recv.at[j],
-            device(z_to, x_to, 2 * h_to + low_to, h),
+            device(z, x_to, 2 * h_to + low_to, h),
         ), pltpu.make_async_copy(src, dst, rhs_recv.at[j])
 
     chip = 4 * x + 2 * low + h
 
-    def rhs_stays(j, c_to):
-        return jnp.logical_and(j == 0, jnp.logical_and(c_to == chip, q == h))
+    def rhs_stays(c_to):
+        return jnp.logical_and(c_to == chip, q == h)
 
     for j in range(2):
 
@@ -129,7 +145,7 @@
         def _(step, j=j):
             c_to = (step + chip) % 16
             away, home = rhs_copy(j, c_to)
-            stays = rhs_stays(j, c_to)
+            stays = rhs_stays(c_to)
 
             @pl.when(stays)
             def _():
@@ -145,29 +161,19 @@
     is_diag = col % 8 == row
     diag_slot = col // 8
 
-    move = remote(own.at[1], moved, move_send, move_recv, device(3 - z, x, y, q))
-    move_needed = col <= 8 + row
-    moved_needed = col <= 14 - 2 * z + h
-    early = jnp.logical_and(move_needed, jnp.logical_not(jnp.logical_and(is_diag, diag_slot == 1)))
-    late = jnp.logical_and(is_diag, diag_slot == 1)
-
-    @pl.when(early)
-    def _():
-        move.start()
-
-
-    def sends(piece, k, dx, dy):
-        par = (k // 2 + k) % 2
-        first_is_y = piece % 2 == 0
-        da, db = (dy, dx) if first_is_y else (dx, dy)
-        on_line = db == 0
-        first_plus = jnp.logical_and(on_line, jnp.logical_or(da == 0, jnp.logical_and(da == 1, par == 0)))
-        first_minus = jnp.logical_and(on_line, jnp.logical_or(da == 0, jnp.logical_and(da == 3, par == 1)))
-        second_plus = jnp.logical_or(on_line, jnp.logical_and(db == 1, par == 0))
-        second_minus = jnp.logical_or(on_line, jnp.logical_and(db == 3, par == 1))
-        if first_is_y:
-            return second_plus, second_minus, first_plus, first_minus
-        return first_plus, first_minus, second_plus, second_minus
+    def edges(piece, k, dx, dy):
+        ways = {0: (dx, (k % 2)), 2: (dy, ((k + k // 2) % 2))}
+        first = 2 if FIRST_Y[piece] else 0
+        gap, par = ways[first]
+        on_line = ways[2 - first][0] == 0
+        flags = {
+            first: on_line & ((gap == 0) | ((gap == 1) & (par == 0))),
+            first + 1: on_line & ((gap == 0) | ((gap == 3) & (par == 1))),
+        }
+        gap, par = ways[2 - first]
+        flags[2 - first] = (gap == 0) | ((gap == 1) & (par == 0))
+        flags[3 - first] = (gap == 0) | ((gap == 3) & (par == 1))
+        return flags
 
     def neighbour(way, core):
         if way == 0:
@@ -182,7 +188,7 @@
         return pl.ds(piece * part, part)
 
     def source_copies(j):
-        src = own.at[0] if j == 0 else moved
+        src = own.at[j]
         for piece in range(PIECES):
             for way in range(5):
                 target = neighbour(way, h) if way < 4 else device(z, x, y, h)
@@ -206,7 +212,7 @@
 
         @pl.when(q == h)
         def _():
-            grid[j, col] = own[0] if j == 0 else moved[...]
+            grid[j, col] = own[j]
 
     def source_wait(j):
         for way, copy in source_copies(j):
@@ -218,73 +224,76 @@
                 def _(copy=copy):
                     copy.wait_send()
 
-    source_first = col <= row
-
-    @pl.when(jnp.logical_and(source_first, jnp.logical_not(is_diag)))
-    def _():
-        source(0)
+    needed = (col <= row, col <= 8 + row)
+    diag_first = is_diag & (diag_slot == 0)
+    diag_second = is_diag & (diag_slot == 1)
+
+    pl.when(needed[0] & jnp.logical_not(diag_first))(lambda: source(0))
 
     @pl.when(is_diag)
     def _():
         invert(own.at[diag_slot], inverse)
         own[diag_slot] = inverse[...]
 
-    @pl.when(late)
-    def _():
-        move.start()
-
-    @pl.when(jnp.logical_and(source_first, is_diag))
-    def _():
-        source(0)
-
-    def passing(j, k, do):
-        dx = (x - k // 4 + 4) % 4
-        dy = (y - 2 * q - (k // 2) % 2 + 4) % 4
-        at_source = jnp.logical_and(dx == 0, dy == 0)
-        is_source = jnp.logical_and(at_source, k % 2 == q)
-        for piece in range(PIECES):
-            spot = grid.at[j, k, rows_of(piece), :]
-            copies = [
-                remote(spot, spot, pass_send.at[j, k, piece, way], grid_recv.at[j, k, piece], neighbour(way, q))
-                for way in range(4)
-            ]
-            flags = sends(piece, k, dx, dy)
-            if do == "pass":
-
-                @pl.when(jnp.logical_not(is_source))
-                def _(copies=copies):
-                    copies[0].wait_recv()
-
-            for way in range(4):
-
-                @pl.when(jnp.logical_and(flags[way], jnp.logical_not(at_source)))
-                def _(copy=copies[way]):
+    pl.when(diag_first)(lambda: source(0))
+    pl.when(needed[1])(lambda: source(1))
+
+    reach = (0, 1, 2, 1)
+    offsets = sorted(((dx, dy) for dx in range(4) for dy in range(4)), key=lambda o: reach[o[0]] + reach[o[1]])
+
+    def offset_of(n):
+        dx = dy = jnp.int32(0)
+        for i, (a, b) in enumerate(offsets):
+            dx, dy = jnp.where(n == i, a, dx), jnp.where(n == i, b, dy)
+        return dx, dy
+
+    def number_of(dx, dy):
+        n = jnp.int32(0)
+        for i, (a, b) in enumerate(offsets):
+            n = jnp.where((dx == a) & (dy == b), i, n)
+        return n
+
+    def passing(j, n, limit, do, after=None):
+        dx, dy = offset_of(n)
+        x_from, y_from = (x - dx + 4) % 4, (y - dy + 4) % 4
+        away = n > 0
+        for side in range(2):
+            k = 4 * x_from + 2 * (y_from % 2) + side
+
+            @pl.when((y_from // 2 == q) & (k <= limit))
+            def _(k=k, side=side):
+                for piece in range(PIECES):
+                    spot = grid.at[j, k, rows_of(piece), :]
+
+                    def copy(way, spot=spot, piece=piece):
+                        return remote(spot, spot, pass_send.at[j, k, piece, way], grid_recv.at[j, k, piece], neighbour(way, q))
+
                     if do == "pass":
-                        copy.start()
-                    else:
-                        copy.wait_send()
-
-    @pl.loop(0, first_row + 1)
-    def _(k):
-        passing(0, k, "pass")
-
-    @pl.when(moved_needed)
-    def _():
-        move.wait_recv()
-        source(1)
-
-    @pl.loop(0, second_row + 1)
-    def _(k):
-        passing(1, k, "pass")
+                        pl.when(away | (q != side))(lambda copy=copy: copy(0).wait_recv())
+                    for way, flag in edges(piece, k, dx, dy).items():
+
+                        @pl.when(flag & away)
+                        def _(copy=copy, way=way):
+                            if do == "pass":
+                                copy(way).start()
+                            else:
+                                copy(way).wait_send()
+
+                if after is not None:
+                    after(k)
+
+    @pl.loop(0, 16)
+    def _(n):
+        passing(0, n, first_row, "pass")
 
     for j in range(2):
         remote(state.at[j], state.at[j], rhs_send.at[j, 0], rhs_recv.at[j], here).wait_recv()
 
     def owner_z(k):
-        return jnp.where(k < 8, k // 2, 7 - k // 2)
+        return (k % 8) // 2
 
     def wanted(k, z_to):
-        return jnp.logical_or(k < 8, z_to < owner_z(k))
+        return (k < 8) | (z_to > owner_z(k))
 
     def solved_copies(k):
         spot = solved.at[k]
@@ -301,8 +310,8 @@
 
     def out_copy(k):
         spot = out.at[pl.ds(pl.multiple_of((k // 8) * nb, nb), nb), :]
-        stays = jnp.logical_and(k < 8, h == q)
-        target = device((k % 8) // 2, x, 2 * q + low, h)
+        stays = h == q
+        target = device(z, x, 2 * q + low, h)
         away = remote(solved.at[k], spot, out_send.at[k // 8], out_recv.at[k // 8], target)
         home = pltpu.make_async_copy(solved.at[k], spot, out_recv.at[k // 8])
         return stays, away, home
@@ -320,46 +329,56 @@
         other_core = jnp.logical_and(same_chip, jnp.logical_and(k % 2 != q, jnp.logical_or(k % 2 == 0, k < 8)))
         return jnp.logical_or(other_core, jnp.logical_and(jnp.logical_not(same_chip), wanted(k, z)))
 
-    @pl.loop(0, 16)
+    def solve(k):
+        slot = k // 8
+        solved[k] = product(grid[slot, k], state[slot])
+        for flag, copy in solved_copies(k):
+            pl.when(flag)(copy.start)
+        stays, away, home = out_copy(k)
+        pl.when(stays)(home.start)
+        pl.when(jnp.logical_not(stays))(away.start)
+
+    def update(slot, k):
+        state[slot] = state[slot] - product(grid[slot, k], solved[k])
+
+    span = 7 + 2 * z
+
+    def passed(k):
+        return jnp.minimum((16 * k) // span, 16)
+
+    @pl.loop(-1, 16)
     def _(k):
-        slot = k // 8
-
-        @pl.when(is_owner(k))
-        def _():
-            solved[k] = product(grid[slot, k], state[slot])
-            for flag, copy in solved_copies(k):
-
-                @pl.when(flag)
-                def _(copy=copy):
-                    copy.start()
-
-            stays, away, home = out_copy(k)
-
-            @pl.when(stays)
-            def _():
-                home.start()
-
-            @pl.when(jnp.logical_not(stays))
-            def _():
-                away.start()
-
-        @pl.when(gets(k))
+        @pl.when((k >= 0) & gets(k))
         def _():
             spot = solved.at[k]
             remote(spot, spot, solved_pass.at[k], solved_recv.at[k], here).wait_recv()
             flag, copy = pass_to_partner(k)
-
-            @pl.when(flag)
-            def _():
-                copy.start()
-
-        @pl.when(k < first_row)
-        def _():
-            state[0] = state[0] - product(grid[0, k], solved[k])
-
-        @pl.when(k < second_row)
-        def _():
-            state[1] = state[1] - product(grid[1, k], solved[k])
+            pl.when(flag)(copy.start)
+
+        k_y = 2 * q + (k // 2) % 2
+        taken = number_of((x - k // 4 + 4) % 4, (y - k_y + 4) % 4) < passed(k)
+        early = (k >= 0) & (k < first_row)
+        late = (k >= 0) & (k < second_row) & taken
+        near = (k + 1) // 8
+
+        @pl.when(jnp.where(k < 7, early, late) & (k < 15))
+        def _():
+            update(near, k)
+
+        pl.when(is_owner(k + 1) & (k < 15))(lambda: solve(k + 1))
+
+        @pl.when((k < 7) & late)
+        def _():
+            update(1, k)
+
+        @pl.when(k >= 0)
+        def _():
+            def after(column):
+                pl.when((column <= k) & (column < second_row))(lambda: update(1, column))
+
+            @pl.loop(passed(k), passed(k + 1))
+            def _(n):
+                passing(1, n, second_row, "pass", after)
 
     @pl.loop(0, 16)
     def _(k):
@@ -383,25 +402,13 @@
         def _():
             copy.wait_send()
 
-        @pl.when(k <= first_row)
-        def _():
-            passing(0, k, "done")
-
-        @pl.when(k <= second_row)
-        def _():
-            passing(1, k, "done")
-
-    @pl.when(source_first)
-    def _():
-        source_wait(0)
-
-    @pl.when(moved_needed)
-    def _():
-        source_wait(1)
-
-    @pl.when(move_needed)
-    def _():
-        move.wait_send()
+    @pl.loop(0, 16)
+    def _(n):
+        passing(0, n, first_row, "done")
+        passing(1, n, second_row, "done")
+
+    for j in range(2):
+        pl.when(needed[j])(lambda j=j: source_wait(j))
 
     for j in range(2):
 
@@ -409,7 +416,7 @@
         def _(c_to, j=j):
             away, _ = rhs_copy(j, c_to)
 
-            @pl.when(jnp.logical_not(rhs_stays(j, c_to)))
+            @pl.when(jnp.logical_not(rhs_stays(c_to)))
             def _():
                 away.wait_send()
 
@@ -430,14 +437,11 @@
             pltpu.VMEM((2, 16, nb, nb), F32),
             pltpu.VMEM((2, nb, nb), F32),
             pltpu.VMEM((nb, nb), F32),
-            pltpu.VMEM((nb, nb), F32),
             pltpu.VMEM((16, nb, ncol), F32),
             pltpu.VMEM((2, nb, ncol), F32),
             dma((2,)),
             dma((2, 16)),
             dma((2,)),
-            dma,
-            dma,
             dma((2, 16, PIECES)),
             dma((2, PIECES, 5)),
             dma((2, 16, PIECES, 4)),
@@ -448,7 +452,7 @@
             dma((2,)),
         ],
         compiler_params=pltpu.CompilerParams(
-            has_side_effects=True, vmem_limit_bytes=60 * 1024 * 1024
+            collective_id=0, has_side_effects=True, vmem_limit_bytes=60 * 1024 * 1024
         ),
     )(tri, rhs)
 

time: 384 us -> 223 us (0.58)
  the two profiles are of different devices: /device:TPU:27 before, /device:TPU:101 now
where the time goes in v2:
time: 223 us; the launch traced here: 222 us
  Pallas kernels  220 us (99%)
    pallas_call x1, Pallas kernels, on_device(): pl.pallas_call(kernel, out_shape=jax.ShapeDtypeStruct((2 * nb, ncol), F32...  220 us

profile of v2, /device:TPU:101, one launch (start us, length us, event | category | flops | bytes accessed | tf_op | source)
XLA Modules:
  0.0 222.2 jit_solution(5550373125959433690)
XLA Ops:
  0.0 220.3 %shard_map.28 = f32[1024,128]{1,0:T(8,128)} custom-call(f32[1024,512]{1,0:T(8,128)} %tri.1, f32[64,2048]{1,0:T(8,128)} %rhs.1), custom_call_target="tpu_custom_call" | custom-call | tf_op jit(solution)/shard_map/pallas_call | solution.py:431
  220.3 1.9 copy.4

commit v3 on v2

--- a/solution.py
+++ b/solution.py
@@ -162,7 +162,7 @@
     diag_slot = col // 8
 
     def edges(piece, k, dx, dy):
-        ways = {0: (dx, (k % 2)), 2: (dy, ((k + k // 2) % 2))}
+        ways = {0: (dx, ((k // 4 + 1) // 2 + 1 + (piece // 2) * k) % 2), 2: (dy, (k + k // 2) % 2)}
         first = 2 if FIRST_Y[piece] else 0
         gap, par = ways[first]
         on_line = ways[2 - first][0] == 0
@@ -236,10 +236,8 @@
         own[diag_slot] = inverse[...]
 
     pl.when(diag_first)(lambda: source(0))
-    pl.when(needed[1])(lambda: source(1))
-
     reach = (0, 1, 2, 1)
-    offsets = sorted(((dx, dy) for dx in range(4) for dy in range(4)), key=lambda o: reach[o[0]] + reach[o[1]])
+    offsets = sorted(((dx, dy) for dx in range(4) for dy in range(4)), key=lambda o: (reach[o[0]] + reach[o[1]], o[1], o[0]))
 
     def offset_of(n):
         dx = dy = jnp.int32(0)
@@ -282,9 +280,20 @@
                 if after is not None:
                     after(k)
 
+    ahead = 8 * jnp.maximum(z - 1, 0) // (3 - 1)
+    at_once = z > 1
+
+    pl.when(at_once & needed[1])(lambda: source(1))
+
     @pl.loop(0, 16)
     def _(n):
         passing(0, n, first_row, "pass")
+
+        @pl.loop((n * ahead) // 16, ((n + 1) * ahead) // 16)
+        def _(m):
+            passing(1, m, second_row, "pass")
+
+    pl.when(jnp.logical_not(at_once) & needed[1])(lambda: source(1))
 
     for j in range(2):
         remote(state.at[j], state.at[j], rhs_send.at[j, 0], rhs_recv.at[j], here).wait_recv()
@@ -341,10 +350,8 @@
     def update(slot, k):
         state[slot] = state[slot] - product(grid[slot, k], solved[k])
 
-    span = 7 + 2 * z
-
     def passed(k):
-        return jnp.minimum((16 * k) // span, 16)
+        return jnp.where(k <= 2 * z, ahead, 16)
 
     @pl.loop(-1, 16)
     def _(k):

time: 223 us -> 202 us (0.906)
  Pallas kernels: 220 us -> 200 us
    pallas_call x1, Pallas kernels: 220 us -> 200 us  [on_device(): pl.pallas_call(kernel, out_shape=jax.ShapeDtypeStruct((2 * nb, ncol), F32...]
where the time goes in v3:
time: 202 us
  Pallas kernels  200 us (99%)
    pallas_call x1, Pallas kernels, on_device(): pl.pallas_call(kernel, out_shape=jax.ShapeDtypeStruct((2 * nb, ncol), F32...  200 us

profile of v3, /device:TPU:101, one launch (start us, length us, event | category | flops | bytes accessed | tf_op | source)
XLA Modules:
  0.0 202.3 jit_solution(7211357798859049193)
XLA Ops:
  0.0 200.4 %shard_map.28 = f32[1024,128]{1,0:T(8,128)} custom-call(f32[1024,512]{1,0:T(8,128)} %tri.1, f32[64,2048]{1,0:T(8,128)} %rhs.1), custom_call_target="tpu_custom_call" | custom-call | tf_op jit(solution)/shard_map/pallas_call | solution.py:438
  200.5 1.9 copy.4

commit v4 on v3

--- a/solution.py
+++ b/solution.py
@@ -162,7 +162,7 @@
     diag_slot = col // 8
 
     def edges(piece, k, dx, dy):
-        ways = {0: (dx, ((k // 4 + 1) // 2 + 1 + (piece // 2) * k) % 2), 2: (dy, (k + k // 2) % 2)}
+        ways = {0: (dx, k % 2), 2: (dy, (k + k // 2) % 2)}
         first = 2 if FIRST_Y[piece] else 0
         gap, par = ways[first]
         on_line = ways[2 - first][0] == 0
@@ -187,12 +187,21 @@
     def rows_of(piece):
         return pl.ds(piece * part, part)
 
+    def shifts(j, piece):
+        return (z >= 2) & (j == 0) & (piece >= PIECES // 2)
+
     def source_copies(j):
         src = own.at[j]
         for piece in range(PIECES):
-            for way in range(5):
-                target = neighbour(way, h) if way < 4 else device(z, x, y, h)
-                yield way, remote(
+            shifted = shifts(j, piece)
+            for way in range(6):
+                if way < 4:
+                    target, flag = neighbour(way, h), jnp.logical_not(shifted)
+                elif way == 4:
+                    target, flag = device(z, x, y, h), jnp.logical_not(shifted) & (q != h)
+                else:
+                    target, flag = device(z, (x + 2) % 4, y, h), shifted
+                yield flag, remote(
                     src.at[rows_of(piece), :],
                     grid.at[j, col, rows_of(piece), :],
                     source_send.at[j, piece, way],
@@ -201,28 +210,18 @@
                 )
 
     def source(j):
-        for way, copy in source_copies(j):
-            if way < 4:
-                copy.start()
-            else:
-
-                @pl.when(q != h)
-                def _(copy=copy):
-                    copy.start()
-
-        @pl.when(q == h)
-        def _():
-            grid[j, col] = own[j]
+        for flag, copy in source_copies(j):
+            pl.when(flag)(copy.start)
+
+        for piece in range(PIECES):
+
+            @pl.when((q == h) & jnp.logical_not(shifts(j, piece)))
+            def _(piece=piece):
+                grid[j, col, rows_of(piece), :] = own[j, rows_of(piece), :]
 
     def source_wait(j):
-        for way, copy in source_copies(j):
-            if way < 4:
-                copy.wait_send()
-            else:
-
-                @pl.when(q != h)
-                def _(copy=copy):
-                    copy.wait_send()
+        for flag, copy in source_copies(j):
+            pl.when(flag)(copy.wait_send)
 
     needed = (col <= row, col <= 8 + row)
     diag_first = is_diag & (diag_slot == 0)
@@ -257,30 +256,32 @@
         away = n > 0
         for side in range(2):
             k = 4 * x_from + 2 * (y_from % 2) + side
-
-            @pl.when((y_from // 2 == q) & (k <= limit))
-            def _(k=k, side=side):
-                for piece in range(PIECES):
-                    spot = grid.at[j, k, rows_of(piece), :]
-
-                    def copy(way, spot=spot, piece=piece):
-                        return remote(spot, spot, pass_send.at[j, k, piece, way], grid_recv.at[j, k, piece], neighbour(way, q))
+            for piece in range(PIECES):
+                shifted = shifts(j, piece)
+                k_piece = jnp.where(shifted, (k + 8) % 16, k)
+
+                @pl.when((y_from // 2 == q) & (k_piece <= limit))
+                def _(k=k, k_piece=k_piece, piece=piece, side=side, shifted=shifted):
+                    spot = grid.at[j, k_piece, rows_of(piece), :]
+
+                    def copy(way):
+                        return remote(spot, spot, pass_send.at[j, k_piece, piece, way], grid_recv.at[j, k_piece, piece], neighbour(way, q))
 
                     if do == "pass":
-                        pl.when(away | (q != side))(lambda copy=copy: copy(0).wait_recv())
+                        pl.when(away | (q != side) | shifted)(lambda: copy(0).wait_recv())
                     for way, flag in edges(piece, k, dx, dy).items():
 
-                        @pl.when(flag & away)
-                        def _(copy=copy, way=way):
+                        @pl.when(flag & (away | shifted))
+                        def _(way=way):
                             if do == "pass":
                                 copy(way).start()
                             else:
                                 copy(way).wait_send()
 
-                if after is not None:
-                    after(k)
-
-    ahead = 8 * jnp.maximum(z - 1, 0) // (3 - 1)
+            if after is not None:
+                pl.when((y_from // 2 == q) & (k <= limit))(lambda k=k: after(k))
+
+    ahead = 6 * jnp.maximum(z - 1, 0) // 2
     at_once = z > 1
 
     pl.when(at_once & needed[1])(lambda: source(1))
@@ -351,7 +352,7 @@
         state[slot] = state[slot] - product(grid[slot, k], solved[k])
 
     def passed(k):
-        return jnp.where(k <= 2 * z, ahead, 16)
+        return jnp.where(k <= 2 * z, ahead, jnp.minimum(jnp.maximum(10 + k - 2 * z, ahead), 16))
 
     @pl.loop(-1, 16)
     def _(k):
@@ -450,7 +451,7 @@
             dma((2, 16)),
             dma((2,)),
             dma((2, 16, PIECES)),
-            dma((2, PIECES, 5)),
+            dma((2, PIECES, 6)),
             dma((2, 16, PIECES, 4)),
             dma((16, 4)),
             dma((16,)),

time: 202 us -> 196 us (0.970)
  the two profiles are of different devices: /device:TPU:101 before, /device:TPU:109 now
where the time goes in v4:
time: 196 us
  Pallas kernels  194 us (99%)
    pallas_call x1, Pallas kernels, on_device(): pl.pallas_call(kernel, out_shape=jax.ShapeDtypeStruct((2 * nb, ncol), F32...  194 us

profile of v4, /device:TPU:109, one launch (start us, length us, event | category | flops | bytes accessed | tf_op | source)
XLA Modules:
  0.0 196.0 jit_solution(11799801822727736760)
XLA Ops:
  0.0 194.2 %shard_map.28 = f32[1024,128]{1,0:T(8,128)} custom-call(f32[1024,512]{1,0:T(8,128)} %tri.1, f32[64,2048]{1,0:T(8,128)} %rhs.1), custom_call_target="tpu_custom_call" | custom-call | tf_op jit(solution)/shard_map/pallas_call | solution.py:439
  194.2 1.9 copy.4

commit v5 on v4

--- a/solution.py
+++ b/solution.py
@@ -236,7 +236,7 @@
 
     pl.when(diag_first)(lambda: source(0))
     reach = (0, 1, 2, 1)
-    offsets = sorted(((dx, dy) for dx in range(4) for dy in range(4)), key=lambda o: (reach[o[0]] + reach[o[1]], o[1], o[0]))
+    offsets = sorted(((dx, dy) for dx in range(4) for dy in range(4)), key=lambda o: (reach[o[0]] + 1.5 * reach[o[1]], o[1], o[0]))
 
     def offset_of(n):
         dx = dy = jnp.int32(0)

time: 196 us -> 190 us (0.969)
  the two profiles are of different devices: /device:TPU:109 before, /device:TPU:101 now
where the time goes in v5:
time: 190 us; the launch traced here: 189 us
  Pallas kernels  188 us (99%)
    pallas_call x1, Pallas kernels, on_device(): pl.pallas_call(kernel, out_shape=jax.ShapeDtypeStruct((2 * nb, ncol), F32...  188 us

profile of v5, /device:TPU:101, one launch (start us, length us, event | category | flops | bytes accessed | tf_op | source)
XLA Modules:
  0.0 189.5 jit_solution(18201657573908775876)
XLA Ops:
  0.0 187.6 %shard_map.28 = f32[1024,128]{1,0:T(8,128)} custom-call(f32[1024,512]{1,0:T(8,128)} %tri.1, f32[64,2048]{1,0:T(8,128)} %rhs.1), custom_call_target="tpu_custom_call" | custom-call | tf_op jit(solution)/shard_map/pallas_call | solution.py:439
  187.6 1.9 copy.4

commit v6 on v5

--- a/solution.py
+++ b/solution.py
@@ -139,21 +139,24 @@
     def rhs_stays(c_to):
         return jnp.logical_and(c_to == chip, q == h)
 
-    for j in range(2):
-
-        @pl.loop(0, 16)
-        def _(step, j=j):
-            c_to = (step + chip) % 16
-            away, home = rhs_copy(j, c_to)
-            stays = rhs_stays(c_to)
-
-            @pl.when(stays)
-            def _():
-                home.start()
-
-            @pl.when(jnp.logical_not(stays))
-            def _():
-                away.start()
+    def send_rhs():
+        for j in range(2):
+
+            @pl.loop(0, 16)
+            def _(step, j=j):
+                c_to = (step + chip) % 16
+                away, home = rhs_copy(j, c_to)
+                stays = rhs_stays(c_to)
+
+                @pl.when(stays)
+                def _():
+                    home.start()
+
+                @pl.when(jnp.logical_not(stays))
+                def _():
+                    away.start()
+
+    pl.when(z < 2)(send_rhs)
 
     for load in loads:
         load.wait()
@@ -285,6 +288,7 @@
     at_once = z > 1
 
     pl.when(at_once & needed[1])(lambda: source(1))
+    pl.when(z >= 2)(send_rhs)
 
     @pl.loop(0, 16)
     def _(n):

time: 190 us -> 190 us (level)
  no operation moved by 1% of the time
where the time goes in v6:
time: 190 us; the launch traced here: 189 us
  Pallas kernels  188 us (99%)
    pallas_call x1, Pallas kernels, on_device(): pl.pallas_call(kernel, out_shape=jax.ShapeDtypeStruct((2 * nb, ncol), F32...  188 us

profile of v6, /device:TPU:101, one launch (start us, length us, event | category | flops | bytes accessed | tf_op | source)
XLA Modules:
  0.0 189.5 jit_solution(6549178472697354102)
XLA Ops:
  0.0 187.6 %shard_map.28 = f32[1024,128]{1,0:T(8,128)} custom-call(f32[1024,512]{1,0:T(8,128)} %tri.1, f32[64,2048]{1,0:T(8,128)} %rhs.1), custom_call_target="tpu_custom_call" | custom-call | tf_op jit(solution)/shard_map/pallas_call | solution.py:443
  187.6 1.9 copy.4
